TPU v7x, 32 devices: a whole 2x2x4 slice. The times are simulated.
32 devices in a mesh: dp: 4 (over x, core), expert: 8 (over z, y).
Axes of the slice: x: 2, y: 2, z: 4, core: 2. Of those that a mesh axis runs over, the one named last changes fastest.
Arguments:
- tokens: bfloat16 [128, 256, 1280], P(('dp', 'expert')), may hold values from -32 to 32
- slot_keys: bfloat16 [1280, 8], replicated, may hold values from -20 to 20
- logit_scale: float32 [1], replicated, may hold values from 8 to 16
- up_weight: bfloat16 [8, 1280, 5120], P('expert', None, 'dp'), may hold values from -0.15625 to 0.15625
- up_bias: bfloat16 [8, 5120], P('expert', 'dp'), may hold values from -3 to 3
- down_weight: bfloat16 [8, 5120, 1280], P('expert', 'dp'), may hold values from -0.078125 to 0.078125
- down_bias: bfloat16 [8, 1280], replicated, may hold values from -3 to 3
Outputs:
- mixed_out: bfloat16 [128, 256, 1280], P(('dp', 'expert'))
All inputs are finite; a program needn't handle non-finite values.
Results may differ from a plain program's by a relative error of at most 0.017.
Values may be sent and summed in bfloat16 or wider, within the bound.
A program may use at most 64 MiB of HBM per device.

v0:
```python
import jax
import jax.numpy as jnp
from jax import lax
from jax.sharding import PartitionSpec as P

norm_eps = 1e-06


def unit_rms(values, axis_pos):
    return values * lax.rsqrt(jnp.mean(values * values, axis=axis_pos, keepdims=True) + norm_eps)


def body(tokens, slot_keys, logit_scale, up_weight, up_bias, down_weight, down_bias):
    images = tokens.shape[0]
    patches = tokens.shape[1]
    width = tokens.shape[2]
    per_owner = up_weight.shape[0]
    owners = lax.axis_size("expert")
    normed_tok = unit_rms(tokens.astype(jnp.float32), 2).astype(jnp.bfloat16)
    normed_keys = unit_rms(slot_keys.astype(jnp.float32), 0).astype(jnp.bfloat16)
    raw_scores = jnp.einsum(
        "ipd,dn->inp", normed_tok, normed_keys, preferred_element_type=jnp.float32
    )
    logits = logit_scale[0] * raw_scores / width
    dispatch = jax.nn.softmax(logits, axis=2).astype(jnp.bfloat16)
    combine = jax.nn.softmax(logits, axis=1).astype(jnp.bfloat16)
    slot_inputs = jnp.einsum(
        "inp,ipd->ind", dispatch, tokens, preferred_element_type=jnp.float32
    ).astype(jnp.bfloat16)
    routed = lax.all_to_all(slot_inputs, "expert", split_axis=1, concat_axis=0, tiled=True)
    pre = jnp.einsum(
        "rkd,kdf->rkf",
        lax.all_gather(routed, "dp", axis=0, tiled=True),
        up_weight,
        preferred_element_type=jnp.float32,
    )
    pre = pre + up_bias.astype(jnp.float32)[None]
    hidden = jax.nn.gelu(pre, approximate=False).astype(jnp.bfloat16)
    summed = lax.psum_scatter(
        jnp.einsum("rkf,kfd->rkd", hidden, down_weight, preferred_element_type=jnp.float32).astype(
            jnp.bfloat16
        ),
        "dp",
        scatter_dimension=0,
        tiled=True,
    ).astype(jnp.float32)
    own_bias = lax.dynamic_slice_in_dim(
        down_bias, lax.axis_index("expert") * per_owner, per_owner, 0
    ).astype(jnp.float32)
    finished = (
        (summed + own_bias[None]).astype(jnp.bfloat16).reshape(owners, images, per_owner, width)
    )
    returned = lax.all_to_all(finished, "expert", split_axis=0, concat_axis=0, tiled=True)
    weights = combine.reshape(images, owners, per_owner, patches)
    mixed_out = jnp.einsum("iekp,eikd->ipd", weights, returned, preferred_element_type=jnp.float32)
    return mixed_out.astype(jnp.bfloat16)


def solution(mesh):
    return jax.shard_map(
        body,
        mesh=mesh,
        in_specs=(
            P(("dp", "expert"), None, None),
            P(),
            P(),
            P("expert", None, "dp"),
            P("expert", "dp"),
            P("expert", "dp", None),
            P(),
        ),
        out_specs=P(("dp", "expert"), None, None),
        check_vma=False,
    )
```

profile of v0, /device:TPU:0, one launch (start us, length us, event | category | flops | bytes accessed | tf_op | source)
XLA Modules:
  0.0 83.9 jit_solution(10107239753829949492)
XLA Ops:
  6.5 0.0 copy-start
  7.3 1.0 %fusion.96 = f32[8]{0:T(128)S(1)} fusion(bf16[1280,8]{0,1:T(8,128)(2,1)} %param.8), kind=kLoop, calls=%fused_computation.87 | loop fusion | flops 30712 | bytes 20512 | tf_op jit(solution)/shard_map/reduce_sum | solution.py:10
  8.4 2.3 %fusion.2 = f32[4,256]{1,0:T(4,128)S(1)} fusion(bf16[4,256,1280]{2,1,0:T(8,128)(2,1)} %param.7), kind=kLoop, calls=%fused_computation.4 | loop fusion | flops 3931136 | bytes 2625536 | tf_op jit(solution)/shard_map/reduce_sum | solution.py:10
  10.7 0.0 copy-start.1
  10.7 2.6 %fusion.33 = f32[4,8,256]{2,1,0:T(8,128)S(1)} fusion(bf16[4,256,1280]{2,1,0:T(8,128)(2,1)} %param.7, f32[4,256]{1,0:T(4,128)S(1)} %add_rsqrt_fusion, bf16[1280,8]{0,1:T(8,128)(2,1)} %param.8, f32[8]{0:T(128)S(1)} %add_rsqrt_fusion.1, f32[]{:T(128)} %bitcast.139), kind=kOutput, calls=%fused_computation.24 | convolution fusion | flops 24950784 | bytes 2678820 | tf_op jit(solution)/shard_map/ipd,dn->inp/dot_general | solution.py:21
  13.3 0.2 fusion.133
  13.5 2.2 %convolution_convert_fusion.1 = bf16[4,8,1280]{2,1,0:T(8,128)(2,1)S(1)} fusion(bf16[4,256,1280]{2,1,0:T(8,128)(2,1)} %param.7, f32[4,8]{1,0:T(4,128)S(1)} %fusion.133, f32[4,8,256]{2,1,0:T(8,128)S(1)} %fusion.33), kind=kOutput, calls=%fused_computation.17 | convolution fusion | flops 21037344 | bytes 2736256 | tf_op jit(solution)/shard_map/inp,ipd->ind/dot_general | solution.py:27
  15.8 0.7 copy.11
  16.4 7.3 %all-to-all-start = ((bf16[4,8,1280]{2,0,1:T(4,128)(2,1)}), bf16[4,8,1280]{2,0,1:T(4,128)(2,1)S(1)}, u32[]{:S(2)}, u32[]{:S(2)}) async-start(bf16[4,8,1280]{2,0,1:T(4,128)(2,1)} %copy.11), calls=%async_computation | async-start | bytes 163840 | tf_op jit(solution)/shard_map/all_to_all | solution.py:30
  23.7 0.0 reduce-scatter.2.cloned.1.call-start
  23.8 0.0 copy-done.1
  23.8 6.9 %all-to-all-done = bf16[4,8,1280]{2,0,1:T(4,128)(2,1)S(1)} async-done(((bf16[4,8,1280]{2,0,1:T(4,128)(2,1)}), bf16[4,8,1280]{2,0,1:T(4,128)(2,1)S(1)}, u32[]{:S(2)}, u32[]{:S(2)}) %all-to-all-start) | async-done | bytes 81952 | tf_op jit(solution)/shard_map/all_to_all | solution.py:30
  30.8 6.6 %all_gather.3 = bf16[128,1,1280]{2,0,1:T(8,128)(2,1)} all-gather(bf16[32,1,1280]{2,0,1:T(8,128)(2,1)S(1)} %all_to_all.19), channel_id=1, replica_groups=mesh['dp'=4,'expert'=8] {'dp'}, dimensions={0}, use_global_device_ids=true | all-gather | bytes 409600 | tf_op jit(solution)/shard_map/all_gather | solution.py:33
  37.3 0.0 copy-done
  37.3 5.2 %fusion.20 = bf16[128,1,1280]{2,0,1:T(8,128)(2,1)} fusion(bf16[1,1280,1280]{2,1,0:T(8,128)(2,1)S(1)} %copy-done, bf16[1,1280,1280]{2,1,0:T(8,128)(2,1)} %param.10, bf16[128,1,1280]{2,0,1:T(8,128)(2,1)} %all_gather.3, f32[1280]{0:T(1024)S(1)} %convert_reduce_fusion.1), kind=kOutput, calls=%fused_computation.16 | convolution fusion | flops 849838080 | bytes 7214080 | tf_op jit(solution)/shard_map/rkf,kfd->rkd/dot_general | solution.py:40
  42.6 0.0 reduce-scatter.2.cloned.1.call-update
  42.6 0.8 convert_reduce_fusion
  43.3 17.3 %reduce-scatter.2.cloned.1.call-done = bf16[32,1,1280]{2,0,1:T(8,128)(2,1)} async-done(((bf16[128,1,1280]{2,0,1:T(8,128)(2,1)}), bf16[32,1,1280]{2,0,1:T(8,128)(2,1)}) %reduce-scatter.2.cloned.1.call-update) | async-done | bytes 81936 | tf_op jit(solution)/shard_map/reduce_scatter | solution.py:39
  60.6 0.9 %add_convert_fusion = bf16[32,1,1280]{2,0,1:T(8,128)(2,1)S(1)} fusion(bf16[32,1,1280]{2,0,1:T(8,128)(2,1)} %reduce-scatter.2.cloned.1.call-done, f32[1280]{0:T(1024)S(1)} %convert_reduce_fusion), kind=kLoop, calls=%fused_computation.82 | loop fusion | flops 122880 | bytes 168960 | tf_op jit(solution)/shard_map/convert_element_type | solution.py:51
  61.5 0.7 reshape.56
  62.2 5.5 %all-to-all-start.1 = ((bf16[8,4,1,1280]{3,1,2,0:T(4,128)(2,1)}), bf16[8,4,1,1280]{3,1,2,0:T(4,128)(2,1)S(1)}, u32[]{:S(2)}, u32[]{:S(2)}) async-start(bf16[8,4,1,1280]{3,1,2,0:T(4,128)(2,1)} %bitcast.16), calls=%async_computation.2 | async-start | bytes 163840 | tf_op jit(solution)/shard_map/all_to_all | solution.py:53
  67.7 7.0 %all-to-all-done.1 = bf16[8,4,1,1280]{3,1,2,0:T(4,128)(2,1)S(1)} async-done(((bf16[8,4,1,1280]{3,1,2,0:T(4,128)(2,1)}), bf16[8,4,1,1280]{3,1,2,0:T(4,128)(2,1)S(1)}, u32[]{:S(2)}, u32[]{:S(2)}) %all-to-all-start.1) | async-done | bytes 81952 | tf_op jit(solution)/shard_map/all_to_all | solution.py:53
  74.7 2.4 %convolution_convert_fusion = bf16[4,256,1280]{2,1,0:T(8,128)(2,1)} fusion(bf16[8,4,1,1280]{3,1,2,0:T(4,128)(2,1)S(1)} %all-to-all-done.1, f32[4,256]{1,0:T(4,128)S(1)} %fusion.134, f32[4,8,256]{2,1,0:T(8,128)S(1)} %fusion.33), kind=kOutput, calls=%fused_computation.6 | convolution fusion | flops 22307848 | bytes 2740224 | tf_op jit(solution)/shard_map/iekp,eikd->ipd/dot_general | solution.py:55
  (5 shorter events, 0.1 us)
Async XLA Ops:
  6.5 30.8 %copy-start = (bf16[1,1280,1280]{2,1,0:T(8,128)(2,1)S(1)}, bf16[1,1280,1280]{2,1,0:T(8,128)(2,1)}, u32[]{:S(2)}) copy-start(bf16[1,1280,1280]{2,1,0:T(8,128)(2,1)} %param.12) | copy-start | bytes 9830404
  10.7 13.1 %copy-start.1 = (bf16[1,1280]{1,0:T(2,128)(2,1)S(1)}, bf16[1,1280]{1,0:T(2,128)(2,1)}, u32[]{:S(2)}) copy-start(bf16[1,1280]{1,0:T(2,128)(2,1)} %param.11) | copy-start | bytes 7684
  16.4 14.3 %all-to-all-start = ((bf16[4,8,1280]{2,0,1:T(4,128)(2,1)}), bf16[4,8,1280]{2,0,1:T(4,128)(2,1)S(1)}, u32[]{:S(2)}, u32[]{:S(2)}) async-start(bf16[4,8,1280]{2,0,1:T(4,128)(2,1)} %copy.11), calls=%async_computation | async-start | bytes 163840 | tf_op jit(solution)/shard_map/all_to_all | solution.py:30
  23.7 36.9 %reduce-scatter.2.cloned.1.call-start = ((), (), s32[]{:S(2)}) async-start(), calls=%async_computation.3 | async-start | bytes 409600 | tf_op jit(solution)/shard_map/reduce_scatter | solution.py:39
  62.2 12.5 %all-to-all-start.1 = ((bf16[8,4,1,1280]{3,1,2,0:T(4,128)(2,1)}), bf16[8,4,1,1280]{3,1,2,0:T(4,128)(2,1)S(1)}, u32[]{:S(2)}, u32[]{:S(2)}) async-start(bf16[8,4,1,1280]{3,1,2,0:T(4,128)(2,1)} %bitcast.16), calls=%async_computation.2 | async-start | bytes 163840 | tf_op jit(solution)/shard_map/all_to_all | solution.py:53
Sparse Core Ops, SparseCore 0:
  42.7 17.8 reduce-scatter.1
where the time goes:
time: 84.4 us; the launch traced here: 83.9 us
  waiting for transfers between devices  31.2 us (37%)
  between operations  14.2 us (17%)
  starting transfers between devices  12.8 us (15%)
  matrix products  12.5 us (15%)
  blocking collectives  6.55 us (8%)
  other arithmetic  5.26 us (6%)
  local copies, waits for them, and re-layouts  1.37 us (2%)
    reduce_scatter x1, waiting for transfers between devices, body(): lax.psum_scatter(jnp.einsum('rkf,kfd->rkd', hidden, down_weight, preferre...  17.3 us
    all_to_all x1, starting transfers between devices, body(): lax.all_to_all(slot_inputs, 'expert', split_axis=1, concat_axis=0, tiled=...  7.31 us
    all_to_all x1, waiting for transfers between devices, body(): lax.all_to_all(finished, 'expert', split_axis=0, concat_axis=0, tiled=True)  6.98 us
    all_to_all x1, waiting for transfers between devices, body(): lax.all_to_all(slot_inputs, 'expert', split_axis=1, concat_axis=0, tiled=...  6.93 us
    all_gather x1, blocking collectives, body(): lax.all_gather(routed, 'dp', axis=0, tiled=True)  6.55 us
    all_to_all x1, starting transfers between devices, body(): lax.all_to_all(finished, 'expert', split_axis=0, concat_axis=0, tiled=True)  5.5 us
    dot_general x1, matrix products, body(): jnp.einsum('rkf,kfd->rkd', hidden, down_weight, preferred_element_type=jn...  5.22 us
    reduce_sum x2, other arithmetic, unit_rms(): jnp.mean(values * values, axis=axis_pos, keepdims=True) + norm_eps  3.35 us
  transfers between devices with their start and end apart: 3, of which 3 were waited for; matrix products, arithmetic and copies ran while one was open for 1% of the time, Pallas kernels for 0%

commit v1 on v0

--- a/solution.py
+++ b/solution.py
@@ -27,7 +27,12 @@
     slot_inputs = jnp.einsum(
         "inp,ipd->ind", dispatch, tokens, preferred_element_type=jnp.float32
     ).astype(jnp.bfloat16)
-    routed = lax.all_to_all(slot_inputs, "expert", split_axis=1, concat_axis=0, tiled=True)
+    routed = jnp.concatenate(
+        lax.all_to_all(
+            jnp.stack(jnp.split(slot_inputs, lax.axis_size("expert"), axis=1)), "expert", 0, 0
+        ),
+        axis=0,
+    )
     pre = jnp.einsum(
         "rkd,kdf->rkf",
         lax.all_gather(routed, "dp", axis=0, tiled=True),

time: 84.4 us -> 88.7 us (1.051)
  local copies, waits for them, and re-layouts: 1.37 us -> 5.67 us
    unnamed x4 -> x11, local copies, waits for them, and re-layouts: 0.01 us -> 4.24 us
where the time goes in v1:
time: 88.7 us; the launch traced here: 88.2 us
  waiting for transfers between devices  31.2 us (35%)
  between operations  14.3 us (16%)
  starting transfers between devices  12.8 us (14%)
  matrix products  12.5 us (14%)
  blocking collectives  6.55 us (7%)
  local copies, waits for them, and re-layouts  5.67 us (6%)
  other arithmetic  5.26 us (6%)
    reduce_scatter x1, waiting for transfers between devices, body(): lax.psum_scatter(jnp.einsum('rkf,kfd->rkd', hidden, down_weight, preferre...  17.3 us
    all_to_all x1, starting transfers between devices, body(): lax.all_to_all(jnp.stack(jnp.split(slot_inputs, lax.axis_size('expert'),...  7.31 us
    all_to_all x1, waiting for transfers between devices, body(): lax.all_to_all(finished, 'expert', split_axis=0, concat_axis=0, tiled=True)  6.98 us
    all_to_all x1, waiting for transfers between devices, body(): lax.all_to_all(jnp.stack(jnp.split(slot_inputs, lax.axis_size('expert'),...  6.93 us
    all_gather x1, blocking collectives, body(): lax.all_gather(routed, 'dp', axis=0, tiled=True)  6.55 us
    all_to_all x1, starting transfers between devices, body(): lax.all_to_all(finished, 'expert', split_axis=0, concat_axis=0, tiled=True)  5.5 us
    dot_general x1, matrix products, body(): jnp.einsum('rkf,kfd->rkd', hidden, down_weight, preferred_element_type=jn...  5.22 us
    unnamed x11, local copies, waits for them, and re-layouts  4.24 us
  transfers between devices with their start and end apart: 3, of which 3 were waited for; matrix products, arithmetic and copies ran while one was open for 1% of the time, Pallas kernels for 0%

profile of v1, /device:TPU:0, one launch (start us, length us, event | category | flops | bytes accessed | tf_op | source)
XLA Modules:
  0.0 88.2 jit_solution(1371782699578867841)
XLA Ops:
  6.5 0.0 copy-start
  7.3 1.0 %fusion.96 = f32[8]{0:T(128)S(1)} fusion(bf16[1280,8]{0,1:T(8,128)(2,1)} %param.8), kind=kLoop, calls=%fused_computation.87 | loop fusion | flops 30712 | bytes 20512 | tf_op jit(solution)/shard_map/reduce_sum | solution.py:10
  8.4 2.3 %fusion.2 = f32[4,256]{1,0:T(4,128)S(1)} fusion(bf16[4,256,1280]{2,1,0:T(8,128)(2,1)} %param.7), kind=kLoop, calls=%fused_computation.4 | loop fusion | flops 3931136 | bytes 2625536 | tf_op jit(solution)/shard_map/reduce_sum | solution.py:10
  10.7 0.0 copy-start.1
  10.7 2.6 %fusion.33 = f32[4,8,256]{2,1,0:T(8,128)S(1)} fusion(bf16[4,256,1280]{2,1,0:T(8,128)(2,1)} %param.7, f32[4,256]{1,0:T(4,128)S(1)} %add_rsqrt_fusion, bf16[1280,8]{0,1:T(8,128)(2,1)} %param.8, f32[8]{0:T(128)S(1)} %add_rsqrt_fusion.1, f32[]{:T(128)} %bitcast.152), kind=kOutput, calls=%fused_computation.24 | convolution fusion | flops 24950784 | bytes 2678820 | tf_op jit(solution)/shard_map/ipd,dn->inp/dot_general | solution.py:21
  13.3 0.2 fusion.134
  13.5 2.2 %convolution_convert_fusion.1 = bf16[4,8,1280]{2,1,0:T(8,128)(2,1)S(1)} fusion(bf16[4,256,1280]{2,1,0:T(8,128)(2,1)} %param.7, f32[4,8]{1,0:T(4,128)S(1)} %fusion.134, f32[4,8,256]{2,1,0:T(8,128)S(1)} %fusion.33), kind=kOutput, calls=%fused_computation.17 | convolution fusion | flops 21037344 | bytes 2736256 | tf_op jit(solution)/shard_map/inp,ipd->ind/dot_general | solution.py:27
  15.8 0.1 fusion.133
  15.9 0.6 constant_dynamic-update-slice_fusion.7
  16.5 0.6 constant_dynamic-update-slice_fusion.6
  17.1 0.6 constant_dynamic-update-slice_fusion.5
  17.7 0.6 constant_dynamic-update-slice_fusion.4
  18.3 0.6 constant_dynamic-update-slice_fusion.3
  18.9 0.6 constant_dynamic-update-slice_fusion.2
  19.5 0.6 constant_dynamic-update-slice_fusion.1
  20.1 0.6 constant_dynamic-update-slice_fusion
  20.8 7.3 %all-to-all-start = ((bf16[8,4,1,1280]{3,1,2,0:T(4,128)(2,1)}), bf16[8,4,1,1280]{3,1,2,0:T(4,128)(2,1)S(1)}, u32[]{:S(2)}, u32[]{:S(2)}) async-start(bf16[8,4,1,1280]{3,1,2,0:T(4,128)(2,1)} %constant_dynamic-update-slice_fusion), calls=%async_computation | async-start | bytes 163840 | tf_op jit(solution)/shard_map/all_to_all | solution.py:31
  28.1 0.0 reduce-scatter.2.cloned.1.call-start
  28.1 0.0 copy-done.1
  28.1 6.9 %all-to-all-done = bf16[8,4,1,1280]{3,1,2,0:T(4,128)(2,1)S(1)} async-done(((bf16[8,4,1,1280]{3,1,2,0:T(4,128)(2,1)}), bf16[8,4,1,1280]{3,1,2,0:T(4,128)(2,1)S(1)}, u32[]{:S(2)}, u32[]{:S(2)}) %all-to-all-start) | async-done | bytes 81952 | tf_op jit(solution)/shard_map/all_to_all | solution.py:31
  35.1 6.6 %all_gather.3 = bf16[128,1,1280]{2,0,1:T(8,128)(2,1)} all-gather(bf16[32,1,1280]{2,0,1:T(8,128)(2,1)S(1)} %reshape.55), channel_id=1, replica_groups=mesh['dp'=4,'expert'=8] {'dp'}, dimensions={0}, use_global_device_ids=true | all-gather | bytes 409600 | tf_op jit(solution)/shard_map/all_gather | solution.py:38
  41.7 0.0 copy-done
  41.7 5.2 %fusion.20 = bf16[128,1,1280]{2,0,1:T(8,128)(2,1)} fusion(bf16[1,1280,1280]{2,1,0:T(8,128)(2,1)S(1)} %copy-done, bf16[1,1280,1280]{2,1,0:T(8,128)(2,1)} %param.10, bf16[128,1,1280]{2,0,1:T(8,128)(2,1)} %all_gather.3, f32[1280]{0:T(1024)S(1)} %convert_reduce_fusion.1), kind=kOutput, calls=%fused_computation.16 | convolution fusion | flops 849838080 | bytes 7214080 | tf_op jit(solution)/shard_map/rkf,kfd->rkd/dot_general | solution.py:45
  46.9 0.0 reduce-scatter.2.cloned.1.call-update
  46.9 0.8 convert_reduce_fusion
  47.7 17.3 %reduce-scatter.2.cloned.1.call-done = bf16[32,1,1280]{2,0,1:T(8,128)(2,1)} async-done(((bf16[128,1,1280]{2,0,1:T(8,128)(2,1)}), bf16[32,1,1280]{2,0,1:T(8,128)(2,1)}) %reduce-scatter.2.cloned.1.call-update) | async-done | bytes 81936 | tf_op jit(solution)/shard_map/reduce_scatter | solution.py:44
  64.9 0.9 %add_convert_fusion = bf16[32,1,1280]{2,0,1:T(8,128)(2,1)S(1)} fusion(bf16[32,1,1280]{2,0,1:T(8,128)(2,1)} %reduce-scatter.2.cloned.1.call-done, f32[1280]{0:T(1024)S(1)} %convert_reduce_fusion), kind=kLoop, calls=%fused_computation.82 | loop fusion | flops 122880 | bytes 168960 | tf_op jit(solution)/shard_map/convert_element_type | solution.py:56
  65.8 0.7 reshape.60
  66.5 5.5 %all-to-all-start.1 = ((bf16[8,4,1,1280]{3,1,2,0:T(4,128)(2,1)}), bf16[8,4,1,1280]{3,1,2,0:T(4,128)(2,1)S(1)}, u32[]{:S(2)}, u32[]{:S(2)}) async-start(bf16[8,4,1,1280]{3,1,2,0:T(4,128)(2,1)} %bitcast.14), calls=%async_computation.2 | async-start | bytes 163840 | tf_op jit(solution)/shard_map/all_to_all | solution.py:58
  72.0 7.0 %all-to-all-done.1 = bf16[8,4,1,1280]{3,1,2,0:T(4,128)(2,1)S(1)} async-done(((bf16[8,4,1,1280]{3,1,2,0:T(4,128)(2,1)}), bf16[8,4,1,1280]{3,1,2,0:T(4,128)(2,1)S(1)}, u32[]{:S(2)}, u32[]{:S(2)}) %all-to-all-start.1) | async-done | bytes 81952 | tf_op jit(solution)/shard_map/all_to_all | solution.py:58
  79.0 2.4 %convolution_convert_fusion = bf16[4,256,1280]{2,1,0:T(8,128)(2,1)} fusion(bf16[8,4,1,1280]{3,1,2,0:T(4,128)(2,1)S(1)} %all-to-all-done.1, f32[4,256]{1,0:T(4,128)S(1)} %fusion.135, f32[4,8,256]{2,1,0:T(8,128)S(1)} %fusion.33), kind=kOutput, calls=%fused_computation.6 | convolution fusion | flops 22307848 | bytes 2740224 | tf_op jit(solution)/shard_map/iekp,eikd->ipd/dot_general | solution.py:60
  (5 shorter events, 0.1 us)
Async XLA Ops:
  6.5 35.1 %copy-start = (bf16[1,1280,1280]{2,1,0:T(8,128)(2,1)S(1)}, bf16[1,1280,1280]{2,1,0:T(8,128)(2,1)}, u32[]{:S(2)}) copy-start(bf16[1,1280,1280]{2,1,0:T(8,128)(2,1)} %param.12) | copy-start | bytes 9830404
  10.7 17.4 %copy-start.1 = (bf16[1,1280]{1,0:T(2,128)(2,1)S(1)}, bf16[1,1280]{1,0:T(2,128)(2,1)}, u32[]{:S(2)}) copy-start(bf16[1,1280]{1,0:T(2,128)(2,1)} %param.11) | copy-start | bytes 7684
  20.8 14.3 %all-to-all-start = ((bf16[8,4,1,1280]{3,1,2,0:T(4,128)(2,1)}), bf16[8,4,1,1280]{3,1,2,0:T(4,128)(2,1)S(1)}, u32[]{:S(2)}, u32[]{:S(2)}) async-start(bf16[8,4,1,1280]{3,1,2,0:T(4,128)(2,1)} %constant_dynamic-update-slice_fusion), calls=%async_computation | async-start | bytes 163840 | tf_op jit(solution)/shard_map/all_to_all | solution.py:31
  28.1 36.8 %reduce-scatter.2.cloned.1.call-start = ((), (), s32[]{:S(2)}) async-start(), calls=%async_computation.3 | async-start | bytes 409600 | tf_op jit(solution)/shard_map/reduce_scatter | solution.py:44
  66.5 12.5 %all-to-all-start.1 = ((bf16[8,4,1,1280]{3,1,2,0:T(4,128)(2,1)}), bf16[8,4,1,1280]{3,1,2,0:T(4,128)(2,1)S(1)}, u32[]{:S(2)}, u32[]{:S(2)}) async-start(bf16[8,4,1,1280]{3,1,2,0:T(4,128)(2,1)} %bitcast.14), calls=%async_computation.2 | async-start | bytes 163840 | tf_op jit(solution)/shard_map/all_to_all | solution.py:58
Sparse Core Ops, SparseCore 0:
  47.0 17.8 reduce-scatter.1
